TPU v7x, 32 devices: a whole 2x2x4 slice. The times are simulated.
32 devices in a mesh: section: 4 (over y, x), seq: 8 (over z, core).
Axes of the slice: x: 2, y: 2, z: 4, core: 2. Of those that a mesh axis runs over, the one named last changes fastest.
Arguments:
- queries: bfloat16 [4, 1024, 4096], P('section', 'seq'), may hold values from -500 to 500
- keys: bfloat16 [4, 1024, 512], P('section', 'seq'), may hold values from -6 to 6
- values: bfloat16 [4, 1024, 512], P('section', 'seq'), may hold values from -6 to 6
- out_grad: bfloat16 [4, 1024, 4096], P('section', 'seq'), may hold values from -6 to 6
- documents: int32 [4, 1024], P('section'), may hold values from 0 to 3, never falling along the last dimension, each value on 1 to 512 neighbouring positions
- query_weight: bfloat16 [4, 4096, 4096], P('section', 'seq'), may hold values from -0.09375 to 0.09375
- key_weight: bfloat16 [4, 512, 4096], P('section'), may hold values from -0.1875 to 0.1875
- value_weight: bfloat16 [4, 512, 4096], P('section'), may hold values from -0.1875 to 0.1875
Outputs:
- upstream: bfloat16 [4, 1024, 4096], P('section', 'seq')
Inputs may be any that keep to these rules, and one draw needn't show every extreme that they name: `documents`: each section's document ids never fall along its tokens.
All inputs are finite; a program needn't handle non-finite values.
Results may differ from a plain program's by a relative error of at most 0.0058.
Values may be sent and summed in bfloat16 or wider, within the bound.
A program may use at most 192 MiB of HBM per device.

v0:
```python
import math

import jax
import jax.numpy as jnp
from jax import lax
from jax.sharding import PartitionSpec as P

KV = 4
HD = 128


def passed_along(block, axis, distance):
    devices = range(lax.axis_size(axis))
    route = [(i - distance, i) for i in devices if i - distance in devices]
    return lax.ppermute(block, axis, route)


def body(queries, keys, values, out_grad, documents, query_weight, key_weight, value_weight):
    count = lax.axis_size("seq")
    tok = queries.shape[1]
    total = tok * count
    heads_here = query_weight.shape[1] // HD
    reps = count // KV
    scale = 1.0 / math.sqrt(HD)
    q_send = queries[0].reshape(tok, count, heads_here * HD)
    o_send = out_grad[0].reshape(tok, count, heads_here * HD)
    q_all, o_all = (
        lax.all_to_all(q_send, "seq", split_axis=1, concat_axis=0, tiled=True),
        lax.all_to_all(o_send, "seq", split_axis=1, concat_axis=0, tiled=True),
    )
    q_all = q_all.reshape(total, heads_here, HD)
    o_all = o_all.reshape(total, heads_here, HD)
    k_rep = jnp.repeat(keys[0].reshape(tok, KV, HD), reps, axis=1)
    v_rep = jnp.repeat(values[0].reshape(tok, KV, HD), reps, axis=1)
    k_head, v_head = (
        lax.all_to_all(k_rep, "seq", split_axis=1, concat_axis=0, tiled=True),
        lax.all_to_all(v_rep, "seq", split_axis=1, concat_axis=0, tiled=True),
    )
    k_head = k_head.reshape(total, HD)
    v_head = v_head.reshape(total, HD)
    doc_ids = documents[0]
    block = min(512, total)
    columns = lax.iota(jnp.int32, total)

    def attend(carry, index):
        dkey, dvalue = carry
        first = index * block
        q_blk = lax.dynamic_slice_in_dim(q_all, first, block, 0)
        o_blk = lax.dynamic_slice_in_dim(o_all, first, block, 0)
        rows = first + lax.iota(jnp.int32, block)
        row_ids = lax.dynamic_slice_in_dim(doc_ids, first, block, 0)
        allowed = (columns[None, :] <= rows[:, None]) & (doc_ids[None, :] == row_ids[:, None])
        scores = (
            jnp.einsum("bhd,td->hbt", q_blk, k_head, preferred_element_type=jnp.float32) * scale
        )
        scores = jnp.where(allowed[None], scores, -jnp.inf)
        top = jnp.max(scores, axis=-1, keepdims=True)
        expo = jnp.exp(scores - top)
        prob = expo / jnp.sum(expo, axis=-1, keepdims=True)
        prob_low = prob.astype(jnp.bfloat16)
        dprob = jnp.einsum("bhd,td->hbt", o_blk, v_head, preferred_element_type=jnp.float32)
        delta = jnp.sum(prob * dprob, axis=-1, keepdims=True)
        dscore = (prob * (dprob - delta) * scale).astype(jnp.bfloat16)
        dq_blk = jnp.einsum(
            "hbt,td->bhd", dscore, k_head, preferred_element_type=jnp.float32
        ).astype(jnp.bfloat16)
        dkey = dkey + jnp.einsum("hbt,bhd->td", dscore, q_blk, preferred_element_type=jnp.float32)
        dvalue = dvalue + jnp.einsum(
            "hbt,bhd->td", prob_low, o_blk, preferred_element_type=jnp.float32
        )
        return ((dkey, dvalue), dq_blk)

    start_carry = (jnp.zeros((total, HD), jnp.float32), jnp.zeros((total, HD), jnp.float32))
    (dkey, dvalue), dq_blocks = lax.scan(
        attend, start_carry, jnp.arange(total // block, dtype=jnp.int32)
    )
    dquery = dq_blocks.reshape(total, heads_here * HD)
    dkey_low = dkey.astype(jnp.bfloat16)
    dvalue_low = dvalue.astype(jnp.bfloat16)
    dq_tok, dk_tok, dv_tok = (
        lax.all_to_all(
            dquery.reshape(total, 1, heads_here * HD),
            "seq",
            split_axis=0,
            concat_axis=1,
            tiled=True,
        ),
        lax.all_to_all(
            dkey_low.reshape(total, 1, HD), "seq", split_axis=0, concat_axis=1, tiled=True
        ),
        lax.all_to_all(
            dvalue_low.reshape(total, 1, HD), "seq", split_axis=0, concat_axis=1, tiled=True
        ),
    )
    dq_tok = dq_tok.reshape(tok, count * heads_here * HD)
    dk_tok = dk_tok.reshape(tok, count * HD)
    dv_tok = dv_tok.reshape(tok, count * HD)
    wk_rep = jnp.repeat(key_weight[0].reshape(KV, HD, -1), reps, axis=0).reshape(count * HD, -1)
    wv_rep = jnp.repeat(value_weight[0].reshape(KV, HD, -1), reps, axis=0).reshape(count * HD, -1)
    start_sum = jnp.dot(dk_tok, wk_rep, preferred_element_type=jnp.float32)
    start_sum = start_sum + jnp.dot(dv_tok, wv_rep, preferred_element_type=jnp.float32)
    dinput = start_sum + jnp.dot(
        dq_tok,
        lax.all_gather(query_weight[0], "seq", axis=0, tiled=True),
        preferred_element_type=jnp.float32,
    )
    dinput = dinput.astype(jnp.bfloat16)
    received = passed_along(dinput, "section", -1)
    return received[None]


def solution(mesh):
    in_specs = (
        P("section", "seq", None),
        P("section", "seq", None),
        P("section", "seq", None),
        P("section", "seq", None),
        P("section", None),
        P("section", "seq", None),
        P("section", None, None),
        P("section", None, None),
    )
    out_specs = P("section", "seq", None)
    return jax.shard_map(body, mesh=mesh, in_specs=in_specs, out_specs=out_specs, check_vma=False)
```

profile of v0, /device:TPU:1, one launch (start us, length us, event | category | flops | bytes accessed | tf_op | source)
XLA Modules:
  0.0 432.1 jit_solution(672726303252246511)
XLA Ops:
  9.0 6.4 %all-to-all-start.3 = ((bf16[128,8,128]{2,0,1:T(8,128)(2,1)}), bf16[128,8,128]{2,0,1:T(8,128)(2,1)S(1)}, u32[]{:S(2)}, u32[]{:S(2)}) async-start(bf16[128,8,128]{2,0,1:T(8,128)(2,1)} %bitcast.11), calls=%async_computation.3 | async-start | bytes 524288 | tf_op jit(solution)/shard_map/all_to_all | solution.py:37
  17.6 6.4 %all-to-all-done.3 = bf16[128,8,128]{2,0,1:T(8,128)(2,1)S(1)} async-done(((bf16[128,8,128]{2,0,1:T(8,128)(2,1)}), bf16[128,8,128]{2,0,1:T(8,128)(2,1)S(1)}, u32[]{:S(2)}, u32[]{:S(2)}) %all-to-all-start.3) | async-done | bytes 262176 | tf_op jit(solution)/shard_map/all_to_all | solution.py:37
  24.0 4.6 %all-to-all-start = ((bf16[128,8,512]{0,2,1:T(8,128)(2,1)}), bf16[128,8,512]{0,2,1:T(8,128)(2,1)S(1)}, u32[]{:S(2)}, u32[]{:S(2)}) async-start(bf16[128,8,512]{0,2,1:T(8,128)(2,1)} %bitcast.1), calls=%async_computation | async-start | bytes 2097152 | tf_op jit(solution)/shard_map/all_to_all | solution.py:28
  29.9 54.2 %all-to-all-done = bf16[128,8,512]{0,2,1:T(8,128)(2,1)S(1)} async-done(((bf16[128,8,512]{0,2,1:T(8,128)(2,1)}), bf16[128,8,512]{0,2,1:T(8,128)(2,1)S(1)}, u32[]{:S(2)}, u32[]{:S(2)}) %all-to-all-start) | async-done | bytes 1048608 | tf_op jit(solution)/shard_map/all_to_all | solution.py:28
  84.1 3.8 all-to-all-start.2
  88.0 58.0 %all-to-all-done.2 = bf16[128,8,512]{0,2,1:T(8,128)(2,1)S(1)} async-done(((bf16[128,8,512]{0,2,1:T(8,128)(2,1)}), bf16[128,8,512]{0,2,1:T(8,128)(2,1)S(1)}, u32[]{:S(2)}, u32[]{:S(2)}) %all-to-all-start.2) | async-done | bytes 1048608 | tf_op jit(solution)/shard_map/all_to_all | solution.py:29
  157.8 13.5 %all-to-all-done.1 = bf16[128,8,128]{2,0,1:T(8,128)(2,1)S(1)} async-done(((bf16[128,8,128]{2,0,1:T(8,128)(2,1)}), bf16[128,8,128]{2,0,1:T(8,128)(2,1)S(1)}, u32[]{:S(2)}, u32[]{:S(2)}) %all-to-all-start.1) | async-done | bytes 262176 | tf_op jit(solution)/shard_map/all_to_all | solution.py:36
  171.3 114.1 %while.15 = (s32[]{:T(128)}, f32[1024,128]{1,0:T(8,128)}, f32[1024,128]{1,0:T(8,128)}, bf16[2,512,4,128]{3,2,1,0:T(4,128)(2,1)}, s32[2]{0:T(128)S(1)}, /*index=5...) while((s32[]{:T(128)}, f32[1024,128]{1,0:T(8,128)}, ...), condition=%wide.region_4.5_spmd.clone, body=%wide.region_0.4_spmd.clone.sunk | while | flops 2728664576 | bytes 95738200 | solution.py:74
  173.0 7.4 %fusion.109 = (f32[4,512]{1,0:T(4,128)S(1)}, f32[4,512,1024]{2,1,0:T(8,128)}) fusion(pred[512,1024]{1,0:T(8,128)(4,1)S(1)} %fusion.108, bf16[1024,4,128]{0,2,1:T(8,128)(2,1)} %get-tuple-element.288, s32[]{:T(128)S(6)} %select_n.30, bf16[1024,128]{1,0:T(8,128)(2,1)S(1)} %get-tuple-element.289), kind=kOutput, calls=%fused_computation.62.clone.1 | convolution fusion | flops 545260544 | bytes 9707524 | tf_op jit(solution)/shard_map/while/body/eval_jaxpr/sub | solution.py:58
  180.4 4.5 %fusion.107 = f32[512,4,1024]{2,0,1:T(8,128)} fusion(bf16[1024,4,128]{0,2,1:T(8,128)(2,1)S(1)} %get-tuple-element.290, s32[]{:T(128)S(6)} %select_n.30, bf16[1024,128]{1,0:T(8,128)(2,1)S(1)} %get-tuple-element.291), kind=kOutput, calls=%fused_computation.32.clone.1 | convolution fusion | flops 536870912 | bytes 9175044 | tf_op jit(solution)/shard_map/while/body/eval_jaxpr/bhd,td->hbt/dot_general | solution.py:61
  184.9 16.7 %fusion.112 = bf16[1,512,4,128]{3,1,2,0:T(8,128)(2,1)S(1)} fusion(f32[512,4,1024]{2,0,1:T(8,128)} %fusion.107, bf16[1024,128]{1,0:T(8,128)(2,1)S(1)} %get-tuple-element.289, f32[4,512,1024]{2,1,0:T(8,128)} %get-tuple-element.249, f32[4,512]{1,0:T(4,128)S(1)} %get-tuple-element.250), kind=kOutput, calls=%fused_computation.25.clone.1 | convolution fusion | flops 551816192 | bytes 17571840 | tf_op jit(solution)/shard_map/while/body/eval_jaxpr/hbt,td->bhd/dot_general | solution.py:64
  202.0 6.3 %fusion.111 = f32[1024,128]{1,0:T(8,128)} fusion(f32[1024,128]{1,0:T(8,128)} %get-tuple-element.268, bf16[1024,4,128]{0,2,1:T(8,128)(2,1)S(1)} %get-tuple-element.290, s32[]{:T(128)S(6)} %select_n.30, pred[]{:T(512)S(6)} %compare.3, f32[4,512,1024]{2,1,0:T(8,128)} %get-tuple-element.249, f32[4,512]{1,0:T(4,128)S(1)} %get-tuple-element.250), kind=kOutput, calls=%fused_computation.28.clone.1 | convolution fusion | flops 541327360 | bytes 9969669 | tf_op jit(solution)/shard_map/while/body/eval_jaxpr/hbt,bhd->td/dot_general | solution.py:68
  208.3 19.1 %fusion.110 = f32[1024,128]{1,0:T(8,128)S(1)} fusion(f32[512,4,1024]{2,0,1:T(8,128)} %fusion.107, f32[1024,128]{1,0:T(8,128)S(1)} %copy-done.5, bf16[1024,4,128]{0,2,1:T(8,128)(2,1)} %get-tuple-element.288, s32[]{:T(128)S(6)} %select_n.30, pred[]{:T(512)S(6)} %compare.3, f32[4,512,1024]{2,1,0:T(8,128)} %get-tuple-element.249, ...), kind=kOutput, calls=%fused_computation.29.clone.1 | convolution fusion | flops 551816192 | bytes 35143684 | tf_op jit(solution)/shard_map/while/body/eval_jaxpr/hbt,bhd->td/dot_general | solution.py:67
  230.0 7.4 %fusion.109 = (f32[4,512]{1,0:T(4,128)S(1)}, f32[4,512,1024]{2,1,0:T(8,128)}) fusion(pred[512,1024]{1,0:T(8,128)(4,1)S(1)} %fusion.108, bf16[1024,4,128]{0,2,1:T(8,128)(2,1)} %get-tuple-element.288, s32[]{:T(128)S(6)} %select_n.30, bf16[1024,128]{1,0:T(8,128)(2,1)S(1)} %get-tuple-element.289), kind=kOutput, calls=%fused_computation.62.clone.1 | convolution fusion | flops 545260544 | bytes 9707524 | tf_op jit(solution)/shard_map/while/body/eval_jaxpr/sub | solution.py:58
  237.4 4.5 %fusion.107 = f32[512,4,1024]{2,0,1:T(8,128)} fusion(bf16[1024,4,128]{0,2,1:T(8,128)(2,1)S(1)} %get-tuple-element.290, s32[]{:T(128)S(6)} %select_n.30, bf16[1024,128]{1,0:T(8,128)(2,1)S(1)} %get-tuple-element.291), kind=kOutput, calls=%fused_computation.32.clone.1 | convolution fusion | flops 536870912 | bytes 9175044 | tf_op jit(solution)/shard_map/while/body/eval_jaxpr/bhd,td->hbt/dot_general | solution.py:61
  241.9 16.6 %fusion.112 = bf16[1,512,4,128]{3,1,2,0:T(8,128)(2,1)S(1)} fusion(f32[512,4,1024]{2,0,1:T(8,128)} %fusion.107, bf16[1024,128]{1,0:T(8,128)(2,1)S(1)} %get-tuple-element.289, f32[4,512,1024]{2,1,0:T(8,128)} %get-tuple-element.249, f32[4,512]{1,0:T(4,128)S(1)} %get-tuple-element.250), kind=kOutput, calls=%fused_computation.25.clone.1 | convolution fusion | flops 551816192 | bytes 17571840 | tf_op jit(solution)/shard_map/while/body/eval_jaxpr/hbt,td->bhd/dot_general | solution.py:64
  259.0 6.5 %fusion.111 = f32[1024,128]{1,0:T(8,128)} fusion(f32[1024,128]{1,0:T(8,128)} %get-tuple-element.268, bf16[1024,4,128]{0,2,1:T(8,128)(2,1)S(1)} %get-tuple-element.290, s32[]{:T(128)S(6)} %select_n.30, pred[]{:T(512)S(6)} %compare.3, f32[4,512,1024]{2,1,0:T(8,128)} %get-tuple-element.249, f32[4,512]{1,0:T(4,128)S(1)} %get-tuple-element.250), kind=kOutput, calls=%fused_computation.28.clone.1 | convolution fusion | flops 541327360 | bytes 9969669 | tf_op jit(solution)/shard_map/while/body/eval_jaxpr/hbt,bhd->td/dot_general | solution.py:68
  265.5 19.1 %fusion.110 = f32[1024,128]{1,0:T(8,128)S(1)} fusion(f32[512,4,1024]{2,0,1:T(8,128)} %fusion.107, f32[1024,128]{1,0:T(8,128)S(1)} %copy-done.5, bf16[1024,4,128]{0,2,1:T(8,128)(2,1)} %get-tuple-element.288, s32[]{:T(128)S(6)} %select_n.30, pred[]{:T(512)S(6)} %compare.3, f32[4,512,1024]{2,1,0:T(8,128)} %get-tuple-element.249, ...), kind=kOutput, calls=%fused_computation.29.clone.1 | convolution fusion | flops 551816192 | bytes 35143684 | tf_op jit(solution)/shard_map/while/body/eval_jaxpr/hbt,bhd->td/dot_general | solution.py:67
  293.8 16.8 %all-to-all-done.4 = bf16[8,2,8192]{2,1,0:T(2,128)(2,1)S(1)} async-done(((bf16[8,2,8192]{2,1,0:T(2,128)(2,1)}), bf16[8,2,8192]{2,1,0:T(2,128)(2,1)S(1)}, u32[]{:S(2)}, u32[]{:S(2)}) %all-to-all-start.4) | async-done | bytes 262176 | tf_op jit(solution)/shard_map/all_to_all | solution.py:88
  310.6 4.2 all-to-all-start.5
  314.8 5.9 %reshape_reshape.12 = bf16[1024,1,512]{2,1,0:T(2,128)(2,1)S(1)} reshape(bf16[2,512,4,128]{3,2,1,0:T(4,128)(2,1)} %get-tuple-element.71) | data formatting | bytes 2097152 | tf_op jit(solution)/shard_map/reshape;reshape | solution.py:82
  320.7 6.9 %reduce.2 = bf16[1024,512]{1,0:T(8,128)(2,1)S(1)} reduce(bf16[1024,1,512]{2,1,0:T(2,128)(2,1)S(1)} %reshape_reshape.12, bf16[]{:T(256)} %broadcast.93), dimensions={1}, to_apply=%reshape_reshape.12.reduce_sub_computation | reduce | bytes 2097154 | tf_op jit(solution)/shard_map/reshape;reshape | solution.py:82
  329.2 8.1 %all-to-all-done.5 = bf16[8,2,8192]{2,1,0:T(2,128)(2,1)} async-done(((bf16[8,2,8192]{2,1,0:T(2,128)(2,1)}), bf16[8,2,8192]{2,1,0:T(2,128)(2,1)}, u32[]{:S(2)}, u32[]{:S(2)}) %all-to-all-start.5) | async-done | bytes 262176 | tf_op jit(solution)/shard_map/all_to_all | solution.py:91
  337.3 4.5 %all-to-all-start.6 = ((bf16[8,2,32768]{2,1,0:T(2,128)(2,1)}), bf16[8,2,32768]{2,1,0:T(2,128)(2,1)}, u32[]{:S(2)}, u32[]{:S(2)}) async-start(bf16[8,2,32768]{2,1,0:T(2,128)(2,1)} %reshape.126), calls=%async_computation.6 | async-start | bytes 2097152 | tf_op jit(solution)/shard_map/all_to_all | solution.py:81
  344.4 6.5 %broadcast_in_dim.44 = bf16[4,2,128,4096]{3,2,1,0:T(8,128)(2,1)} broadcast(bf16[4,128,4096]{2,1,0:T(8,128)(2,1)} %bitcast.171), dimensions={0,2,3} | broadcast | bytes 12582912 | tf_op jit(solution)/shard_map/broadcast_in_dim | solution.py:98
  350.9 4.8 %fusion.79 = f32[128,4096]{1,0:T(8,128)S(1)} fusion(bf16[128,1024]{0,1:T(8,128)(2,1)S(1)} %bitcast.177, bf16[1024,4096]{1,0:T(8,128)(2,1)} %bitcast.168), kind=kOutput, calls=%fused_computation.63 | convolution fusion | flops 1073741824 | bytes 10747904 | tf_op jit(solution)/shard_map/dot_general | solution.py:100
  355.8 4.3 broadcast_in_dim.45
  360.0 6.1 %convolution_add_fusion = f32[128,4096]{1,0:T(8,128)} fusion(f32[128,4096]{1,0:T(8,128)S(1)} %fusion.79, bf16[128,1024]{0,1:T(8,128)(2,1)S(1)} %bitcast.178, bf16[1024,4096]{1,0:T(8,128)(2,1)} %bitcast.167), kind=kOutput, calls=%fused_computation.58 | convolution fusion | flops 1074266112 | bytes 12845056 | tf_op jit(solution)/shard_map/dot_general | solution.py:101
  366.1 13.3 %all-to-all-done.6 = bf16[8,2,32768]{2,1,0:T(2,128)(2,1)} async-done(((bf16[8,2,32768]{2,1,0:T(2,128)(2,1)}), bf16[8,2,32768]{2,1,0:T(2,128)(2,1)}, u32[]{:S(2)}, u32[]{:S(2)}) %all-to-all-start.6) | async-done | bytes 1048608 | tf_op jit(solution)/shard_map/all_to_all | solution.py:81
  379.4 4.3 %reshape.127 = bf16[1024,1,512]{2,1,0:T(2,128)(2,1)S(1)} reshape(bf16[8,2,32768]{2,1,0:T(2,128)(2,1)} %all-to-all-done.6) | data formatting | bytes 2097152
  384.7 13.8 %fusion.67 = bf16[128,4096]{1,0:T(8,128)(2,1)S(1)} fusion(f32[128,4096]{1,0:T(8,128)} %convolution_add_fusion, bf16[128,4096]{0,1:T(8,128)(2,1)S(1)} %bitcast.170, bf16[1,4096,4096]{2,1,0:T(8,128)(2,1)} %all-gather.3.cloned.1.call-done), kind=kOutput, calls=%fused_computation.59 | convolution fusion | flops 4296015872 | bytes 37748736 | tf_op jit(solution)/shard_map/dot_general | solution.py:102
  399.8 24.5 %collective-permute-done = bf16[128,4096]{1,0:T(8,128)(2,1)S(1)} collective-permute-done((bf16[128,4096]{1,0:T(8,128)(2,1)S(1)}, bf16[128,4096]{1,0:T(8,128)(2,1)S(1)}, u32[]{:S(2)}, u32[]{:S(2)}) %collective-permute-start) | collective-permute-done | bytes 1048608 | tf_op jit(solution)/shard_map/ppermute | solution.py:15
  (74 shorter events, 38.4 us)
Async XLA Ops:
  6.5 22.0 %copy-start.4 = (bf16[1,128,4096]{2,1,0:T(8,128)(2,1)S(1)}, bf16[1,128,4096]{2,1,0:T(8,128)(2,1)}, u32[]{:S(2)}) copy-start(bf16[1,128,4096]{2,1,0:T(8,128)(2,1)} %param.13) | copy-start | bytes 3145732
  6.5 81.4 %copy-start.8 = (bf16[1,128,512]{2,1,0:T(8,128)(2,1)S(1)}, bf16[1,128,512]{2,1,0:T(8,128)(2,1)}, u32[]{:S(2)}) copy-start(bf16[1,128,512]{2,1,0:T(8,128)(2,1)} %param.11) | copy-start | bytes 393220
  6.5 378.1 %all-gather.3.cloned.1.call-start = ((), (), s32[]{:S(2)}) async-start(), calls=%async_computation.7 | async-start | bytes 37748736 | tf_op jit(solution)/shard_map/all_gather | solution.py:104
  9.0 15.0 %all-to-all-start.3 = ((bf16[128,8,128]{2,0,1:T(8,128)(2,1)}), bf16[128,8,128]{2,0,1:T(8,128)(2,1)S(1)}, u32[]{:S(2)}, u32[]{:S(2)}) async-start(bf16[128,8,128]{2,0,1:T(8,128)(2,1)} %bitcast.11), calls=%async_computation.3 | async-start | bytes 524288 | tf_op jit(solution)/shard_map/all_to_all | solution.py:37
  17.6 153.7 %copy-start.7 = (s32[1,1024]{1,0:T(1,128)S(1)}, s32[1,1024]{1,0:T(1,128)}, u32[]{:S(2)}) copy-start(s32[1,1024]{1,0:T(1,128)} %param.14) | copy-start | bytes 12292
  24.0 60.1 %all-to-all-start = ((bf16[128,8,512]{0,2,1:T(8,128)(2,1)}), bf16[128,8,512]{0,2,1:T(8,128)(2,1)S(1)}, u32[]{:S(2)}, u32[]{:S(2)}) async-start(bf16[128,8,512]{0,2,1:T(8,128)(2,1)} %bitcast.1), calls=%async_computation | async-start | bytes 2097152 | tf_op jit(solution)/shard_map/all_to_all | solution.py:28
  84.1 61.8 %all-to-all-start.2 = ((bf16[128,8,512]{0,2,1:T(8,128)(2,1)}), bf16[128,8,512]{0,2,1:T(8,128)(2,1)S(1)}, u32[]{:S(2)}, u32[]{:S(2)}) async-start(bf16[128,8,512]{0,2,1:T(8,128)(2,1)} %bitcast.176), calls=%async_computation.2 | async-start | bytes 2097152 | tf_op jit(solution)/shard_map/all_to_all | solution.py:29
  146.7 24.6 %all-to-all-start.1 = ((bf16[128,8,128]{2,0,1:T(8,128)(2,1)}), bf16[128,8,128]{2,0,1:T(8,128)(2,1)S(1)}, u32[]{:S(2)}, u32[]{:S(2)}) async-start(bf16[128,8,128]{2,0,1:T(8,128)(2,1)} %bitcast.4), calls=%async_computation.1 | async-start | bytes 524288 | tf_op jit(solution)/shard_map/all_to_all | solution.py:36
  184.9 16.7 %copy-start.2 = (bf16[2,512,4,128]{3,2,1,0:T(4,128)(2,1)S(1)}, bf16[2,512,4,128]{3,2,1,0:T(4,128)(2,1)}, u32[]{:S(2)}) copy-start(bf16[2,512,4,128]{3,2,1,0:T(4,128)(2,1)} %get-tuple-element.269) | copy-start | bytes 3145732 | tf_op jit(solution)/shard_map/while
  202.0 6.3 %copy-start.3 = (bf16[2,512,4,128]{3,2,1,0:T(4,128)(2,1)}, bf16[2,512,4,128]{3,2,1,0:T(4,128)(2,1)S(1)}, u32[]{:S(2)}) copy-start(bf16[2,512,4,128]{3,2,1,0:T(4,128)(2,1)S(1)} %copy_dynamic-update-slice_fusion.2) | copy-start | bytes 3145732 | tf_op jit(solution)/shard_map/while
  202.0 6.3 %copy-start.5 = (f32[1024,128]{1,0:T(8,128)S(1)}, f32[1024,128]{1,0:T(8,128)}, u32[]{:S(2)}) copy-start(f32[1024,128]{1,0:T(8,128)} %get-tuple-element.267) | copy-start | bytes 1572868 | tf_op jit(solution)/shard_map/while
  227.5 0.8 copy-start.6
  241.9 16.6 %copy-start.2 = (bf16[2,512,4,128]{3,2,1,0:T(4,128)(2,1)S(1)}, bf16[2,512,4,128]{3,2,1,0:T(4,128)(2,1)}, u32[]{:S(2)}) copy-start(bf16[2,512,4,128]{3,2,1,0:T(4,128)(2,1)} %get-tuple-element.269) | copy-start | bytes 3145732 | tf_op jit(solution)/shard_map/while
  258.9 6.5 %copy-start.3 = (bf16[2,512,4,128]{3,2,1,0:T(4,128)(2,1)}, bf16[2,512,4,128]{3,2,1,0:T(4,128)(2,1)S(1)}, u32[]{:S(2)}) copy-start(bf16[2,512,4,128]{3,2,1,0:T(4,128)(2,1)S(1)} %copy_dynamic-update-slice_fusion.2) | copy-start | bytes 3145732 | tf_op jit(solution)/shard_map/while
  259.0 6.5 %copy-start.5 = (f32[1024,128]{1,0:T(8,128)S(1)}, f32[1024,128]{1,0:T(8,128)}, u32[]{:S(2)}) copy-start(f32[1024,128]{1,0:T(8,128)} %get-tuple-element.267) | copy-start | bytes 1572868 | tf_op jit(solution)/shard_map/while
  284.6 0.8 copy-start.6
  288.7 21.9 %all-to-all-start.4 = ((bf16[8,2,8192]{2,1,0:T(2,128)(2,1)}), bf16[8,2,8192]{2,1,0:T(2,128)(2,1)S(1)}, u32[]{:S(2)}, u32[]{:S(2)}) async-start(bf16[8,2,8192]{2,1,0:T(2,128)(2,1)} %reshape.122), calls=%async_computation.4 | async-start | bytes 524288 | tf_op jit(solution)/shard_map/all_to_all | solution.py:88
  310.6 26.7 %all-to-all-start.5 = ((bf16[8,2,8192]{2,1,0:T(2,128)(2,1)}), bf16[8,2,8192]{2,1,0:T(2,128)(2,1)}, u32[]{:S(2)}, u32[]{:S(2)}) async-start(bf16[8,2,8192]{2,1,0:T(2,128)(2,1)} %reshape.124), calls=%async_computation.5 | async-start | bytes 524288 | tf_op jit(solution)/shard_map/all_to_all | solution.py:91
  337.3 42.0 %all-to-all-start.6 = ((bf16[8,2,32768]{2,1,0:T(2,128)(2,1)}), bf16[8,2,32768]{2,1,0:T(2,128)(2,1)}, u32[]{:S(2)}, u32[]{:S(2)}) async-start(bf16[8,2,32768]{2,1,0:T(2,128)(2,1)} %reshape.126), calls=%async_computation.6 | async-start | bytes 2097152 | tf_op jit(solution)/shard_map/all_to_all | solution.py:81
  350.9 4.8 %copy-start = (bf16[1,512,4096]{2,1,0:T(8,128)(2,1)S(1)}, bf16[1,512,4096]{2,1,0:T(8,128)(2,1)}, u32[]{:S(2)}) copy-start(bf16[1,512,4096]{2,1,0:T(8,128)(2,1)} %param.17) | copy-start | bytes 12582916
  355.7 4.3 copy-start.1
  398.5 25.8 %collective-permute-start = (bf16[128,4096]{1,0:T(8,128)(2,1)S(1)}, bf16[128,4096]{1,0:T(8,128)(2,1)S(1)}, u32[]{:S(2)}, u32[]{:S(2)}) collective-permute-start(bf16[128,4096]{1,0:T(8,128)(2,1)S(1)} %fusion.67), channel_id=1, source_target_pairs={{8,0},{16,8},{24,16},{9,1},{17,9},{25,17},{10,2},{18,10},{26,18},{... | collective-permute-start | bytes 3145736 | tf_op jit(solution)/shard_map/ppermute | solution.py:15
Sparse Core Ops, SparseCore 0:
  8.9 375.1 all-gather.2
where the time goes:
time: 435 us; the launch traced here: 432 us
  waiting for transfers between devices  196 us (45%)
  matrix products  133 us (31%)
  local copies, waits for them, and re-layouts  46.3 us (11%)
  starting transfers between devices  32 us (7%)
  between operations  13.6 us (3%)
  other arithmetic  10.6 us (2%)
    all_to_all x1, waiting for transfers between devices, body(): lax.all_to_all(o_send, 'seq', split_axis=1, concat_axis=0, tiled=True)  58 us
    all_to_all x1, waiting for transfers between devices, body(): lax.all_to_all(q_send, 'seq', split_axis=1, concat_axis=0, tiled=True)  54.2 us
    dot_general x2, matrix products, attend(): jnp.einsum('hbt,bhd->td', dscore, q_blk, preferred_element_type=jnp.float32)  38.3 us
    dot_general x2, matrix products, attend(): jnp.einsum('hbt,td->bhd', dscore, k_head, preferred_element_type=jnp.floa...  33.3 us
    ppermute x1, waiting for transfers between devices, passed_along(): return lax.ppermute(block, axis, route)  24.5 us
    all_to_all x1, waiting for transfers between devices, body(): lax.all_to_all(dkey_low.reshape(total, 1, HD), 'seq', split_axis=0, conca...  16.8 us
    sub x2, matrix products, attend(): expo = jnp.exp(scores - top)  14.8 us
    unnamed x22, local copies, waits for them, and re-layouts  13.8 us
  transfers between devices with their start and end apart: 9, of which 8 were waited for; matrix products, arithmetic and copies ran while one was open for 40% of the time, Pallas kernels for 0%

commit v1 on v0

v1 whole, which is shorter than its diff:
```python
import functools
import math

import jax
import jax.numpy as jnp
from jax import lax
from jax.experimental import pallas as pl
from jax.experimental.pallas import tpu as pltpu
from jax.sharding import PartitionSpec as P

KV = 4
HD = 128
MESH = pl.DeviceIdType.MESH
F32 = jnp.float32
BF16 = jnp.bfloat16


def aligned(index, size):
    return pl.ds(pl.multiple_of(index * size, size), size)


def kernel(dims, q_in, k_in, v_in, o_in, start_ref, wq_in, wk_in, wv_in, out_ref,
           q_all, o_all, k_all, v_all, k_turned, dk_sum, dv_sum, grads, weights,
           right_buf, left_buf, acc, final,
           q_sent, o_sent, k_sent, v_sent, q_got, o_got, kv_got,
           w_local, w_sent, w_got, g_sent, g_got,
           right_sent, right_got, left_sent, left_got, final_sent, final_got):
    sections, count, tok, heads, width, block, cw = dims
    total = tok * count
    chips = count // 2
    rows = 2 * tok
    feats = heads * HD
    half = width // 2
    chunks = half // cw
    scale = 1.0 / math.sqrt(HD)
    to_log2 = scale * math.log2(math.e)
    sec = lax.axis_index("section")
    me = lax.axis_index("seq")
    chip = me // 2
    core = me % 2
    partner = (sec, me + 1 - 2 * core)

    barrier = pltpu.get_barrier_semaphore()

    def greet(device):
        pl.semaphore_signal(barrier, inc=1, device_id=device, device_id_type=MESH)

    for off in range(1, count):
        greet((sec, lax.rem(me + off, count)))
    for p in range(2):
        @pl.when(sec > 0)
        def _():
            greet((sec - 1, 2 * chip + p))

        @pl.when(sec < sections - 1)
        def _():
            greet((sec + 1, 2 * chip + p))
    above = jnp.where(sec > 0, 2, 0)
    below = jnp.where(sec < sections - 1, 2, 0)
    pl.semaphore_wait(barrier, count - 1 + above + below)

    def remote(src, dst, send_sem, recv_sem, device):
        return pltpu.make_async_remote_copy(
            src_ref=src, dst_ref=dst, send_sem=send_sem, recv_sem=recv_sem,
            device_id=device, device_id_type=MESH)

    def kv_copy(off, which):
        peer = lax.rem(me + off, count)
        src, dst, sem = ((k_in, k_all, k_sent), (v_in, v_all, v_sent))[which]
        return remote(src.at[:, aligned(peer * KV // count, HD)], dst.at[aligned(me, tok)],
                      sem.at[off], kv_got.at[which], (sec, peer))

    def qo_copy(off, h, which):
        peer = lax.rem(me + off, count)
        src, dst, sem, got = ((q_in, q_all, q_sent, q_got), (o_in, o_all, o_sent, o_got))[which]
        return remote(src.at[:, aligned(peer * heads + h, HD)], dst.at[h, aligned(me, tok)],
                      sem.at[h, off], got.at[h], (sec, peer))

    def w_copy():
        return remote(wq_in.at[:, aligned(1 - core, half)], weights.at[aligned(core, feats)],
                      w_sent.at[0], w_got.at[0], partner)

    for off in range(1, count):
        kv_copy(off, 0).start()
        kv_copy(off, 1).start()

    def send_head(h, carry):
        for off in range(1, count):
            qo_copy(off, h, 0).start()
            qo_copy(off, h, 1).start()
        return carry

    lax.fori_loop(0, heads, send_head, 0)
    w_copy().start()

    mine = aligned(me, tok)
    own = aligned(me * KV // count, HD)
    pltpu.make_async_copy(k_in.at[:, own], k_all.at[mine], kv_got.at[0]).start()
    pltpu.make_async_copy(v_in.at[:, own], v_all.at[mine], kv_got.at[1]).start()

    def own_head(h, carry):
        cols = aligned(me * heads + h, HD)
        pltpu.make_async_copy(q_in.at[:, cols], q_all.at[h, mine], q_got.at[h]).start()
        pltpu.make_async_copy(o_in.at[:, cols], o_all.at[h, mine], o_got.at[h]).start()
        return carry

    lax.fori_loop(0, heads, own_head, 0)

    my_half = aligned(core, half)
    local = [pltpu.make_async_copy(wq_in.at[:, my_half], weights.at[aligned(core, feats)],
                                   w_local.at[0])]
    for p in range(2):
        g = aligned((2 * chip + p) * KV // count, HD)
        base = 2 * feats + p * HD
        local.append(pltpu.make_async_copy(
            wk_in.at[g, my_half], weights.at[base:base + HD], w_local.at[1 + p]))
        local.append(pltpu.make_async_copy(
            wv_in.at[g, my_half], weights.at[base + 2 * HD:base + 3 * HD], w_local.at[3 + p]))
    for copy in local:
        copy.start()

    @pl.when(sec == sections - 1)
    def _():
        out_ref[...] = jnp.zeros_like(out_ref)

    dk_sum[...] = jnp.zeros_like(dk_sum)
    dv_sum[...] = jnp.zeros_like(dv_sum)

    pltpu.make_async_copy(k_all, k_all, kv_got.at[0]).wait()
    pltpu.make_async_copy(v_all, v_all, kv_got.at[1]).wait()
    k_turned[...] = k_all[...].T

    def grad_copy(col, index):
        here = grads.at[:, col]
        return remote(here, here, g_sent.at[index], g_got.at[index], partner)

    def head_cols(p, h):
        return aligned(p * heads + h, HD)

    def tail_cols(p, which):
        return aligned(2 * heads + 2 * which + p, HD)

    def attend(h, carry):
        pltpu.make_async_copy(q_all.at[h], q_all.at[h], q_got.at[h]).wait()
        pltpu.make_async_copy(o_all.at[h], o_all.at[h], o_got.at[h]).wait()
        cols = head_cols(core, h)
        for i in range(total // block):
            lo, hi = i * block, (i + 1) * block
            q = q_all[h, lo:hi, :]
            o = o_all[h, lo:hi, :]
            last = (((1,), (1,)), ((), ()))
            s = lax.dot_general(k_all[:hi], q, last, preferred_element_type=F32)
            dp = lax.dot_general(v_all[:hi], o, last, preferred_element_type=F32)
            j = lax.broadcasted_iota(jnp.int32, (hi, block), 0)
            at = lax.broadcasted_iota(jnp.int32, (hi, block), 1) + lo
            allowed = (j >= start_ref[:, lo:hi]) & (j <= at)
            s = jnp.where(allowed, s, -jnp.inf)
            top = jnp.max(s, axis=0, keepdims=True)
            e = jnp.exp2((s - top) * to_log2)
            inv = 1.0 / jnp.sum(e, axis=0, keepdims=True)
            delta = jnp.sum(e * dp, axis=0, keepdims=True) * inv
            p_low = (e * inv).astype(BF16)
            ds = (e * (dp - delta) * (inv * scale)).astype(BF16)
            dv_sum[:hi] += jnp.dot(p_low, o, preferred_element_type=F32)
            dk_sum[:hi] += jnp.dot(ds, q, preferred_element_type=F32)
            dq = jnp.dot(k_turned[:, :hi], ds, preferred_element_type=F32)
            grads[lo:hi, cols] = dq.T.astype(BF16)
        grad_copy(cols, h).start()
        return carry

    lax.fori_loop(0, heads, attend, 0)
    grads[:, tail_cols(core, 0)] = dk_sum[...].astype(BF16)
    grads[:, tail_cols(core, 1)] = dv_sum[...].astype(BF16)
    for which in range(2):
        grad_copy(tail_cols(core, which), heads + which).start()
    for copy in local:
        copy.wait()
    remote(wq_in.at[:, my_half], weights.at[aligned(1 - core, feats)],
           w_sent.at[0], w_got.at[0], partner).wait_recv()
    for h in range(heads):
        grad_copy(head_cols(1 - core, h), h).wait_recv()
    for which in range(2):
        grad_copy(tail_cols(1 - core, which), heads + which).wait_recv()

    def right_copy(d, k):
        here = right_buf.at[d, k]
        return remote(here, here, right_sent.at[d, k], right_got.at[d, k],
                      (sec, jnp.minimum(me + 2, count - 2 + core)))

    def left_copy(d, k):
        here = left_buf.at[d, k]
        return remote(here, here, left_sent.at[d, k], left_got.at[d, k],
                      (sec, jnp.maximum(me - 2, core)))

    def final_copy(k, p):
        return remote(final.at[k, p * tok:(p + 1) * tok],
                      out_ref.at[:, aligned(core * chunks + k, cw)],
                      final_sent.at[k, p], final_got.at[core, k],
                      (jnp.maximum(sec - 1, 0), 2 * chip + p))

    def product(d, k):
        return jnp.dot(grads[aligned(d, rows), :], weights[:, aligned(k, cw)],
                       preferred_element_type=F32)

    def pass_on(d, k, buf, copy, first):
        acc[...] = product(d, k)

        @pl.when(jnp.logical_not(first))
        def _():
            copy(d, k).wait_recv()
            buf[d, k] = (acc[...] + buf[d, k].astype(F32)).astype(BF16)

        @pl.when(first)
        def _():
            buf[d, k] = acc[...].astype(BF16)

        copy(d, k).start()

    def finish(k):
        acc[...] = product(chip, k)

        @pl.when(chip > 0)
        def _():
            right_copy(chip, k).wait_recv()
            acc[...] += right_buf[chip, k].astype(F32)

        @pl.when(chip < chips - 1)
        def _():
            left_copy(chip, k).wait_recv()
            acc[...] += left_buf[chip, k].astype(F32)

        final[k] = acc[...].astype(BF16)

        @pl.when(sec > 0)
        def _():
            final_copy(k, 0).start()
            final_copy(k, 1).start()

    lag = min(2, chunks)

    def step(k, carry):
        @pl.when(k < chunks)
        def _():
            def to_right(i, c):
                pass_on(chips - 1 - i, k, right_buf, right_copy, chip == 0)
                return c

            def to_left(i, c):
                pass_on(i, k, left_buf, left_copy, chip == chips - 1)
                return c

            lax.fori_loop(0, chips - 1 - chip, to_right, 0)
            lax.fori_loop(0, chip, to_left, 0)

        @pl.when(k >= lag)
        def _():
            finish(k - lag)

        return carry

    lax.fori_loop(0, chunks + lag, step, 0)

    for off in range(1, count):
        kv_copy(off, 0).wait_send()
        kv_copy(off, 1).wait_send()

    def sent_head(h, carry):
        for off in range(1, count):
            qo_copy(off, h, 0).wait_send()
            qo_copy(off, h, 1).wait_send()
        grad_copy(head_cols(core, h), h).wait_send()
        return carry

    lax.fori_loop(0, heads, sent_head, 0)
    for which in range(2):
        grad_copy(tail_cols(core, which), heads + which).wait_send()
    w_copy().wait_send()

    def drain(k, carry):
        def right_done(i, c):
            right_copy(chips - 1 - i, k).wait_send()
            return c

        def left_done(i, c):
            left_copy(i, k).wait_send()
            return c

        lax.fori_loop(0, chips - 1 - chip, right_done, 0)
        lax.fori_loop(0, chip, left_done, 0)

        @pl.when(sec > 0)
        def _():
            final_copy(k, 0).wait_send()
            final_copy(k, 1).wait_send()

        @pl.when(sec < sections - 1)
        def _():
            for p in range(2):
                remote(final.at[k, :tok], out_ref.at[:, aligned(p * chunks + k, cw)],
                       final_sent.at[k, p], final_got.at[p, k], partner).wait_recv()

        return carry

    lax.fori_loop(0, chunks, drain, 0)


def body(queries, keys, values, out_grad, documents, query_weight, key_weight, value_weight):
    sections = lax.axis_size("section")
    count = lax.axis_size("seq")
    tok = queries.shape[1]
    total = tok * count
    feats = query_weight.shape[1]
    heads = feats // HD
    width = query_weight.shape[2]
    chips = count // 2
    rows = 2 * tok
    block = min(256, total)
    cw = min(256, width // 2)
    chunks = width // 2 // cw
    ids = documents[0]
    start = jnp.sum((ids[:, None] < ids[None, :]).astype(jnp.int32), axis=0, keepdims=True)
    dma = pltpu.SemaphoreType.DMA
    deep = 2 * feats + 4 * HD
    anywhere = pl.BlockSpec(memory_space=pl.ANY)
    vmem = pl.BlockSpec(memory_space=pltpu.VMEM)
    out = pl.pallas_call(
        functools.partial(kernel, (sections, count, tok, heads, width, block, cw)),
        out_shape=jax.ShapeDtypeStruct((tok, width), BF16),
        in_specs=[anywhere] * 4 + [vmem] + [anywhere] * 3,
        out_specs=vmem,
        scratch_shapes=[
            pltpu.VMEM((heads, total, HD), BF16),
            pltpu.VMEM((heads, total, HD), BF16),
            pltpu.VMEM((total, HD), BF16),
            pltpu.VMEM((total, HD), BF16),
            pltpu.VMEM((HD, total), BF16),
            pltpu.VMEM((total, HD), F32),
            pltpu.VMEM((total, HD), F32),
            pltpu.VMEM((total, deep), BF16),
            pltpu.VMEM((deep, width // 2), BF16),
            pltpu.VMEM((chips, chunks, rows, cw), BF16),
            pltpu.VMEM((chips, chunks, rows, cw), BF16),
            pltpu.VMEM((rows, cw), F32),
            pltpu.VMEM((chunks, rows, cw), BF16),
            dma((heads, count)),
            dma((heads, count)),
            dma((count,)),
            dma((count,)),
            dma((heads,)),
            dma((heads,)),
            dma((2,)),
            dma((5,)),
            dma((1,)),
            dma((1,)),
            dma((heads + 2,)),
            dma((heads + 2,)),
            dma((chips, chunks)),
            dma((chips, chunks)),
            dma((chips, chunks)),
            dma((chips, chunks)),
            dma((chunks, 2)),
            dma((2, chunks)),
        ],
        compiler_params=pltpu.CompilerParams(
            collective_id=0, has_side_effects=True, vmem_limit_bytes=62 * 1024 * 1024),
        name="attention_back",
    )(queries[0], keys[0], values[0], out_grad[0], start,
      query_weight[0], key_weight[0], value_weight[0])
    return out[None]


def solution(mesh):
    in_specs = (
        P("section", "seq", None),
        P("section", "seq", None),
        P("section", "seq", None),
        P("section", "seq", None),
        P("section", None),
        P("section", "seq", None),
        P("section", None, None),
        P("section", None, None),
    )
    out_specs = P("section", "seq", None)
    return jax.shard_map(body, mesh=mesh, in_specs=in_specs, out_specs=out_specs, check_vma=False)
```

time: 435 us -> 161 us (0.37)
  waiting for transfers between devices: 196 us -> 0 us
  Pallas kernels: 0 us -> 157 us
  matrix products: 133 us -> 0 us
  local copies, waits for them, and re-layouts: 46.3 us -> 2.29 us
  starting transfers between devices: 32 us -> 0 us
  between operations: 13.6 us -> 0.01 us
  other arithmetic: 10.6 us -> 1.83 us
    all_to_all x7 -> x0, waiting for transfers between devices: 170 us -> none  [the longest x1 58 us: body(): lax.all_to_all(o_send, 'seq', split_axis=1, concat_axis=0, tiled=True)]
    pallas_call x0 -> x1, Pallas kernels: none -> 157 us  [body(): pl.pallas_call(functools.partial(kernel, (sections, count, tok, heads, wi...]
    dot_general x11 -> x0, matrix products: 118 us -> none  [the longest x2 38.3 us: attend(): jnp.einsum('hbt,bhd->td', dscore, q_blk, preferred_element_type=jnp.float32)]
    all_to_all x7 -> x0, starting transfers between devices: 30.7 us -> none  [the longest x1 6.37 us: body(): lax.all_to_all(v_rep, 'seq', split_axis=1, concat_axis=0, tiled=True)]
    ppermute x1 -> x0, waiting for transfers between devices: 24.5 us -> none  [passed_along(): return lax.ppermute(block, axis, route)]
    sub x2 -> x0, matrix products: 14.8 us -> none  [attend(): expo = jnp.exp(scores - top)]
    broadcast_in_dim x4 -> x0, local copies, waits for them, and re-layouts: 12.2 us -> none  [the longest x1 6.46 us: body(): jnp.repeat(key_weight[0].reshape(KV, HD, -1), reps, axis=0)]
    unnamed x22 -> x1, local copies, waits for them, and re-layouts: 13.8 us -> 2.29 us
  transfers between devices with their start and end apart: 9 -> 0, of which waited for: 8 -> 0; matrix products, arithmetic and copies ran while one was open for 40% -> 0% of each run, Pallas kernels for 0% -> 0%
where the time goes in v1:
time: 161 us
  Pallas kernels  157 us (98%)
  local copies, waits for them, and re-layouts  2.29 us (1%)
  other arithmetic  1.83 us (1%)
    pallas_call x1, Pallas kernels, body(): pl.pallas_call(functools.partial(kernel, (sections, count, tok, heads, wi...  157 us

profile of v1, /device:TPU:1, one launch (start us, length us, event | category | flops | bytes accessed | tf_op | source)
XLA Modules:
  0.0 161.2 jit_solution(6371460833996419178)
XLA Ops:
  0.0 1.8 %convert_reduce_fusion = s32[1024]{0:T(1024)} fusion(s32[1024]{0:T(1024)} %bitcast.19), kind=kLoop, calls=%fused_computation | loop fusion | flops 3144704 | bytes 8192 | tf_op jit(solution)/shard_map/reduce_sum | solution.py:321
  1.8 157.1 %attention_back.1 = bf16[128,4096]{1,0:T(8,128)(2,1)} custom-call(bf16[128,4096]{1,0:T(8,128)(2,1)} %bitcast.14, bf16[128,512]{1,0:T(8,128)(2,1)} %bitcast.16, bf16[128,512]{1,0:T(8,128)(2,1)} %bitcast.17, bf16[128,4096]{1,0:T(8,128)(2,1)} %bitcast.15, s32[1,1024]{1,0:T(1,128)} %bitcast.18, bf16[512,4096]{1,0:T(8,128)(2,1)} %bitcast.10, ...), custom_call_target="tpu_custom_call" | custom-call | tf_op jit(solution)/shard_map/attention_back/pallas_call | solution.py:326
  158.9 2.3 %copy.10 = bf16[1,128,4096]{2,1,0:T(8,128)(2,1)} copy(bf16[1,128,4096]{2,1,0:T(8,128)(2,1)} %bitcast.13) | data formatting | bytes 2097152

commit v2 on v1

v2 whole, which is shorter than its diff:
```python
import functools
import math

import jax
import jax.numpy as jnp
from jax import lax
from jax.experimental import pallas as pl
from jax.experimental.pallas import tpu as pltpu
from jax.sharding import PartitionSpec as P

KV = 4
HD = 128
MESH = pl.DeviceIdType.MESH
F32 = jnp.float32
BF16 = jnp.bfloat16


def aligned(index, size):
    return pl.ds(pl.multiple_of(index * size, size), size)


def kernel(dims, q_in, k_in, v_in, o_in, start_ref, wq_in, wk_in, wv_in, out_ref,
           q_all, o_all, k_all, v_all, k_turned, dk_sum, dv_sum, grads, weights,
           right_buf, left_buf, acc, final,
           q_sent, o_sent, k_sent, v_sent, q_got, o_got, kv_got,
           w_local, w_sent, w_got, g_sent, g_got,
           right_sent, right_got, left_sent, left_got, final_sent, final_got):
    sections, count, tok, heads, width, cw = dims
    total = tok * count
    chips = count // 2
    rows = 2 * tok
    feats = heads * HD
    span = feats + 2 * HD
    half = width // 2
    chunks = half // cw
    scale = 1.0 / math.sqrt(HD)
    to_log2 = scale * math.log2(math.e)
    sec = lax.axis_index("section")
    me = lax.axis_index("seq")
    chip = me // 2
    core = me % 2
    partner = (sec, me + 1 - 2 * core)

    barrier = pltpu.get_barrier_semaphore()

    def greet(device):
        pl.semaphore_signal(barrier, inc=1, device_id=device, device_id_type=MESH)

    for off in range(1, count):
        greet((sec, lax.rem(me + off, count)))
    for p in range(2):
        @pl.when(sec > 0)
        def _():
            greet((sec - 1, 2 * chip + p))

        @pl.when(sec < sections - 1)
        def _():
            greet((sec + 1, 2 * chip + p))
    above = jnp.where(sec > 0, 2, 0)
    below = jnp.where(sec < sections - 1, 2, 0)
    pl.semaphore_wait(barrier, count - 1 + above + below)

    def remote(src, dst, send_sem, recv_sem, device):
        return pltpu.make_async_remote_copy(
            src_ref=src, dst_ref=dst, send_sem=send_sem, recv_sem=recv_sem,
            device_id=device, device_id_type=MESH)

    def kv_copies(peer):
        head = aligned(peer * KV // count, HD)
        mine = aligned(me, tok)
        return (remote(k_in.at[:, head], k_all.at[mine], k_sent.at[peer], kv_got.at[0],
                       (sec, peer)),
                remote(v_in.at[:, head], v_all.at[mine], v_sent.at[peer], kv_got.at[1],
                       (sec, peer)))

    def qo_copies(peer):
        cols = aligned(peer, feats)
        mine = aligned(core, tok)
        return (remote(q_in.at[:, cols], q_all.at[chip, mine], q_sent.at[peer],
                       q_got.at[chip], (sec, peer)),
                remote(o_in.at[:, cols], o_all.at[chip, mine], o_sent.at[peer],
                       o_got.at[chip], (sec, peer)))

    def w_copy():
        return remote(wq_in.at[:, aligned(1 - core, half)], weights.at[pl.ds(pl.multiple_of(core * span, HD), feats)],
                      w_sent.at[0], w_got.at[0], partner)

    def each_peer(act):
        for far in range(chips - 1, 0, -1):
            for p in range(2):
                @pl.when(chip + far < chips)
                def _():
                    act(2 * (chip + far) + p)

                @pl.when(chip >= far)
                def _():
                    act(2 * (chip - far) + p)
        act(me + 1 - 2 * core)

    def start_both(copies):
        for copy in copies:
            copy.start()

    each_peer(lambda peer: start_both(kv_copies(peer)))
    each_peer(lambda peer: start_both(qo_copies(peer)))
    w_copy().start()

    mine = aligned(me, tok)
    own = aligned(me * KV // count, HD)
    pltpu.make_async_copy(k_in.at[:, own], k_all.at[mine], kv_got.at[0]).start()
    pltpu.make_async_copy(v_in.at[:, own], v_all.at[mine], kv_got.at[1]).start()
    own = aligned(me, feats)
    mine = aligned(core, tok)
    pltpu.make_async_copy(q_in.at[:, own], q_all.at[chip, mine], q_got.at[chip]).start()
    pltpu.make_async_copy(o_in.at[:, own], o_all.at[chip, mine], o_got.at[chip]).start()

    my_half = aligned(core, half)
    my_rows = pl.ds(pl.multiple_of(core * span, HD), feats)
    local = [pltpu.make_async_copy(wq_in.at[:, my_half], weights.at[my_rows], w_local.at[0])]
    for p in range(2):
        g = aligned((2 * chip + p) * KV // count, HD)
        base = p * span + feats
        local.append(pltpu.make_async_copy(
            wk_in.at[g, my_half], weights.at[base:base + HD], w_local.at[1 + p]))
        local.append(pltpu.make_async_copy(
            wv_in.at[g, my_half], weights.at[base + HD:base + 2 * HD], w_local.at[3 + p]))
    for copy in local:
        copy.start()

    @pl.when(sec == sections - 1)
    def _():
        out_ref[...] = jnp.zeros_like(out_ref)

    dk_sum[...] = jnp.zeros_like(dk_sum)
    dv_sum[...] = jnp.zeros_like(dv_sum)

    pltpu.make_async_copy(k_all, k_all, kv_got.at[0]).wait()
    pltpu.make_async_copy(v_all, v_all, kv_got.at[1]).wait()
    k_turned[...] = k_all[...].T

    def grad_copy(b, p):
        here = grads.at[b * rows:(b + 1) * rows, pl.ds(pl.multiple_of(p * span, HD), span)]
        return remote(here, here, g_sent.at[b], g_got.at[b], partner)

    def attend(b):
        lo, hi = b * rows, (b + 1) * rows
        pltpu.make_async_copy(q_all.at[b], q_all.at[b], q_got.at[b]).wait()
        pltpu.make_async_copy(o_all.at[b], o_all.at[b], o_got.at[b]).wait()
        last = (((1,), (1,)), ((), ()))

        def one_head(h, carry):
            q = q_all[b, :, aligned(h, HD)]
            o = o_all[b, :, aligned(h, HD)]
            s = lax.dot_general(k_all[:hi], q, last, preferred_element_type=F32)
            dp = lax.dot_general(v_all[:hi], o, last, preferred_element_type=F32)
            j = lax.broadcasted_iota(jnp.int32, (hi, rows), 0)
            at = lax.broadcasted_iota(jnp.int32, (hi, rows), 1) + lo
            allowed = (j >= start_ref[:, lo:hi]) & (j <= at)
            s = jnp.where(allowed, s, -jnp.inf)
            top = jnp.max(s, axis=0, keepdims=True)
            e = jnp.exp2((s - top) * to_log2)
            inv = 1.0 / jnp.sum(e, axis=0, keepdims=True)
            delta = jnp.sum(e * dp, axis=0, keepdims=True) * inv
            p_low = (e * inv).astype(BF16)
            ds = (e * (dp - delta) * (inv * scale)).astype(BF16)
            dv_sum[:hi] += jnp.dot(p_low, o, preferred_element_type=F32)
            dk_sum[:hi] += jnp.dot(ds, q, preferred_element_type=F32)
            dq = jnp.dot(k_turned[:, :hi], ds, preferred_element_type=F32)
            col = pl.ds(pl.multiple_of(core * span + h * HD, HD), HD)
            grads[lo:hi, col] = dq.T.astype(BF16)
            return carry

        lax.fori_loop(0, heads, one_head, 0)
        tail = core * span + feats
        grads[lo:hi, pl.ds(pl.multiple_of(tail, HD), HD)] = dk_sum[lo:hi].astype(BF16)
        grads[lo:hi, pl.ds(pl.multiple_of(tail + HD, HD), HD)] = dv_sum[lo:hi].astype(BF16)
        grad_copy(b, core).start()

    def right_copy(d, k):
        here = right_buf.at[d, k]
        return remote(here, here, right_sent.at[d, k], right_got.at[d, k],
                      (sec, jnp.minimum(me + 2, count - 2 + core)))

    def left_copy(d, k):
        here = left_buf.at[d, k]
        return remote(here, here, left_sent.at[d, k], left_got.at[d, k],
                      (sec, jnp.maximum(me - 2, core)))

    def final_copy(k, p):
        return remote(final.at[k, p * tok:(p + 1) * tok],
                      out_ref.at[:, aligned(core * chunks + k, cw)],
                      final_sent.at[k, p], final_got.at[core, k],
                      (jnp.maximum(sec - 1, 0), 2 * chip + p))

    def product(d, k):
        return jnp.dot(grads[aligned(d, rows), :], weights[:, aligned(k, cw)],
                       preferred_element_type=F32)

    def set_out(d, buf, copy):
        def one(k, carry):
            buf[d, k] = product(d, k).astype(BF16)
            copy(d, k).start()
            return carry

        lax.fori_loop(0, chunks, one, 0)

    def pass_on(d, k, buf, copy):
        acc[...] = product(d, k)
        copy(d, k).wait_recv()
        buf[d, k] = (acc[...] + buf[d, k].astype(F32)).astype(BF16)
        copy(d, k).start()

    def finish(k):
        acc[...] = product(chip, k)

        @pl.when(chip > 0)
        def _():
            right_copy(chip, k).wait_recv()
            acc[...] += right_buf[chip, k].astype(F32)

        @pl.when(chip < chips - 1)
        def _():
            left_copy(chip, k).wait_recv()
            acc[...] += left_buf[chip, k].astype(F32)

        final[k] = acc[...].astype(BF16)

        @pl.when(sec > 0)
        def _():
            final_copy(k, 0).start()
            final_copy(k, 1).start()

    for b in range(chips - 1, -1, -1):
        attend(b)
        if b == chips - 1:
            for copy in local:
                copy.wait()
            other = pl.ds(pl.multiple_of((1 - core) * span, HD), feats)
            remote(wq_in.at[:, my_half], weights.at[other],
                   w_sent.at[0], w_got.at[0], partner).wait_recv()
        grad_copy(b, 1 - core).wait_recv()
        if b > 0:
            @pl.when(chip == 0)
            def _():
                set_out(b, right_buf, right_copy)
        if b < chips - 1:
            @pl.when(chip == chips - 1)
            def _():
                set_out(b, left_buf, left_copy)

    middle = (chip > 0) & (chip < chips - 1)

    @pl.when(chip > 0)
    def _():
        def one(i, carry):
            pass_on(chips - 1 - i // chunks, i % chunks, right_buf, right_copy)
            return carry

        lax.fori_loop(0, (chips - 1 - chip) * chunks, one, 0)

    def finish_one(k, carry):
        @pl.when(middle)
        def _():
            pass_on(chip - 1, k, left_buf, left_copy)

        finish(k)
        return carry

    lax.fori_loop(0, chunks, finish_one, 0)

    @pl.when(middle)
    def _():
        def one(i, carry):
            pass_on(chip - 2 - i // chunks, i % chunks, left_buf, left_copy)
            return carry

        lax.fori_loop(0, (chip - 1) * chunks, one, 0)

    def sent_both(copies):
        for copy in copies:
            copy.wait_send()

    each_peer(lambda peer: sent_both(kv_copies(peer)))
    each_peer(lambda peer: sent_both(qo_copies(peer)))
    for b in range(chips):
        grad_copy(b, core).wait_send()
    w_copy().wait_send()

    def drain(k, carry):
        def right_done(i, c):
            right_copy(chips - 1 - i, k).wait_send()
            return c

        def left_done(i, c):
            left_copy(i, k).wait_send()
            return c

        lax.fori_loop(0, chips - 1 - chip, right_done, 0)
        lax.fori_loop(0, chip, left_done, 0)

        @pl.when(sec > 0)
        def _():
            final_copy(k, 0).wait_send()
            final_copy(k, 1).wait_send()

        @pl.when(sec < sections - 1)
        def _():
            for p in range(2):
                remote(final.at[k, :tok], out_ref.at[:, aligned(p * chunks + k, cw)],
                       final_sent.at[k, p], final_got.at[p, k], partner).wait_recv()

        return carry

    lax.fori_loop(0, chunks, drain, 0)


def body(queries, keys, values, out_grad, documents, query_weight, key_weight, value_weight):
    sections = lax.axis_size("section")
    count = lax.axis_size("seq")
    tok = queries.shape[1]
    total = tok * count
    feats = query_weight.shape[1]
    heads = feats // HD
    width = query_weight.shape[2]
    chips = count // 2
    rows = 2 * tok
    cw = min(256, width // 2)
    chunks = width // 2 // cw
    ids = documents[0]
    start = jnp.sum((ids[:, None] < ids[None, :]).astype(jnp.int32), axis=0, keepdims=True)
    dma = pltpu.SemaphoreType.DMA
    deep = 2 * feats + 4 * HD
    anywhere = pl.BlockSpec(memory_space=pl.ANY)
    vmem = pl.BlockSpec(memory_space=pltpu.VMEM)
    out = pl.pallas_call(
        functools.partial(kernel, (sections, count, tok, heads, width, cw)),
        out_shape=jax.ShapeDtypeStruct((tok, width), BF16),
        in_specs=[anywhere] * 4 + [vmem] + [anywhere] * 3,
        out_specs=vmem,
        scratch_shapes=[
            pltpu.VMEM((chips, rows, feats), BF16),
            pltpu.VMEM((chips, rows, feats), BF16),
            pltpu.VMEM((total, HD), BF16),
            pltpu.VMEM((total, HD), BF16),
            pltpu.VMEM((HD, total), BF16),
            pltpu.VMEM((total, HD), F32),
            pltpu.VMEM((total, HD), F32),
            pltpu.VMEM((total, deep), BF16),
            pltpu.VMEM((deep, width // 2), BF16),
            pltpu.VMEM((chips, chunks, rows, cw), BF16),
            pltpu.VMEM((chips, chunks, rows, cw), BF16),
            pltpu.VMEM((rows, cw), F32),
            pltpu.VMEM((chunks, rows, cw), BF16),
            dma((count,)),
            dma((count,)),
            dma((count,)),
            dma((count,)),
            dma((chips,)),
            dma((chips,)),
            dma((2,)),
            dma((5,)),
            dma((1,)),
            dma((1,)),
            dma((chips,)),
            dma((chips,)),
            dma((chips, chunks)),
            dma((chips, chunks)),
            dma((chips, chunks)),
            dma((chips, chunks)),
            dma((chunks, 2)),
            dma((2, chunks)),
        ],
        compiler_params=pltpu.CompilerParams(
            collective_id=0, has_side_effects=True, vmem_limit_bytes=62 * 1024 * 1024),
        name="attention_back",
    )(queries[0], keys[0], values[0], out_grad[0], start,
      query_weight[0], key_weight[0], value_weight[0])
    return out[None]


def solution(mesh):
    in_specs = (
        P("section", "seq", None),
        P("section", "seq", None),
        P("section", "seq", None),
        P("section", "seq", None),
        P("section", None),
        P("section", "seq", None),
        P("section", None, None),
        P("section", None, None),
    )
    out_specs = P("section", "seq", None)
    return jax.shard_map(body, mesh=mesh, in_specs=in_specs, out_specs=out_specs, check_vma=False)
```

time: 161 us -> 166 us (1.031)
  Pallas kernels: 157 us -> 161 us
    pallas_call x1, Pallas kernels: 157 us -> 161 us  [body(): pl.pallas_call(functools.partial(kernel, (sections, count, tok, heads, wi...]
where the time goes in v2:
time: 166 us; the launch traced here: 165 us
  Pallas kernels  161 us (97%)
  local copies, waits for them, and re-layouts  2.29 us (1%)
  other arithmetic  1.83 us (1%)
    pallas_call x1, Pallas kernels, body(): pl.pallas_call(functools.partial(kernel, (sections, count, tok, heads, wi...  161 us

profile of v2, /device:TPU:1, one launch (start us, length us, event | category | flops | bytes accessed | tf_op | source)
XLA Modules:
  0.0 165.5 jit_solution(17727655460897897537)
XLA Ops:
  0.0 1.8 %convert_reduce_fusion = s32[1024]{0:T(1024)} fusion(s32[1024]{0:T(1024)} %bitcast.19), kind=kLoop, calls=%fused_computation | loop fusion | flops 3144704 | bytes 8192 | tf_op jit(solution)/shard_map/reduce_sum | solution.py:330
  1.8 161.3 %attention_back.1 = bf16[128,4096]{1,0:T(8,128)(2,1)} custom-call(bf16[128,4096]{1,0:T(8,128)(2,1)} %bitcast.14, bf16[128,512]{1,0:T(8,128)(2,1)} %bitcast.16, bf16[128,512]{1,0:T(8,128)(2,1)} %bitcast.17, bf16[128,4096]{1,0:T(8,128)(2,1)} %bitcast.15, s32[1,1024]{1,0:T(1,128)} %bitcast.18, bf16[512,4096]{1,0:T(8,128)(2,1)} %bitcast.10, ...), custom_call_target="tpu_custom_call" | custom-call | tf_op jit(solution)/shard_map/attention_back/pallas_call | solution.py:335
  163.2 2.3 %copy.10 = bf16[1,128,4096]{2,1,0:T(8,128)(2,1)} copy(bf16[1,128,4096]{2,1,0:T(8,128)(2,1)} %bitcast.13) | data formatting | bytes 2097152

commit v3 on v2

--- a/solution.py
+++ b/solution.py
@@ -19,10 +19,10 @@
     return pl.ds(pl.multiple_of(index * size, size), size)
 
 
-def kernel(dims, q_in, k_in, v_in, o_in, start_ref, wq_in, wk_in, wv_in, out_ref,
-           q_all, o_all, k_all, v_all, k_turned, dk_sum, dv_sum, grads, weights,
+def kernel(dims, q_in, k_in, v_in, o_in, ids_ref, wq_in, wk_in, wv_in, out_ref,
+           q_all, o_all, k_all, v_all, k_turned, dk_sum, dv_sum, start_ref, grads, weights,
            right_buf, left_buf, acc, final,
-           q_sent, o_sent, k_sent, v_sent, q_got, o_got, kv_got,
+           q_sent, o_sent, k_sent, v_sent, q_got, o_got, kv_got, kv_forwarded,
            w_local, w_sent, w_got, g_sent, g_got,
            right_sent, right_got, left_sent, left_got, final_sent, final_got):
     sections, count, tok, heads, width, cw = dims
@@ -68,9 +68,9 @@
     def kv_copies(peer):
         head = aligned(peer * KV // count, HD)
         mine = aligned(me, tok)
-        return (remote(k_in.at[:, head], k_all.at[mine], k_sent.at[peer], kv_got.at[0],
+        return (remote(k_in.at[:, head], k_all.at[mine], k_sent.at[peer], kv_got.at[0, me],
                        (sec, peer)),
-                remote(v_in.at[:, head], v_all.at[mine], v_sent.at[peer], kv_got.at[1],
+                remote(v_in.at[:, head], v_all.at[mine], v_sent.at[peer], kv_got.at[1, me],
                        (sec, peer)))
 
     def qo_copies(peer):
@@ -85,6 +85,17 @@
         return remote(wq_in.at[:, aligned(1 - core, half)], weights.at[pl.ds(pl.multiple_of(core * span, HD), feats)],
                       w_sent.at[0], w_got.at[0], partner)
 
+    def each_twin(act):
+        for far in range(chips - 1, 0, -1):
+            @pl.when(chip + far < chips)
+            def _():
+                act(me + 2 * far)
+
+            @pl.when(chip >= far)
+            def _():
+                act(me - 2 * far)
+        act(me + 1 - 2 * core)
+
     def each_peer(act):
         for far in range(chips - 1, 0, -1):
             for p in range(2):
@@ -101,14 +112,14 @@
         for copy in copies:
             copy.start()
 
-    each_peer(lambda peer: start_both(kv_copies(peer)))
+    each_twin(lambda peer: start_both(kv_copies(peer)))
     each_peer(lambda peer: start_both(qo_copies(peer)))
     w_copy().start()
 
     mine = aligned(me, tok)
     own = aligned(me * KV // count, HD)
-    pltpu.make_async_copy(k_in.at[:, own], k_all.at[mine], kv_got.at[0]).start()
-    pltpu.make_async_copy(v_in.at[:, own], v_all.at[mine], kv_got.at[1]).start()
+    pltpu.make_async_copy(k_in.at[:, own], k_all.at[mine], kv_got.at[0, me]).start()
+    pltpu.make_async_copy(v_in.at[:, own], v_all.at[mine], kv_got.at[1, me]).start()
     own = aligned(me, feats)
     mine = aligned(core, tok)
     pltpu.make_async_copy(q_in.at[:, own], q_all.at[chip, mine], q_got.at[chip]).start()
@@ -134,8 +145,32 @@
     dk_sum[...] = jnp.zeros_like(dk_sum)
     dv_sum[...] = jnp.zeros_like(dv_sum)
 
-    pltpu.make_async_copy(k_all, k_all, kv_got.at[0]).wait()
-    pltpu.make_async_copy(v_all, v_all, kv_got.at[1]).wait()
+    turned = jnp.broadcast_to(ids_ref[...], (HD, total)).T[:, :1]
+    for b in range(chips):
+        before = turned < ids_ref[:, b * rows:(b + 1) * rows]
+        start_ref[:, b * rows:(b + 1) * rows] = jnp.sum(
+            before.astype(jnp.int32), axis=0, keepdims=True)
+
+    def forward(which, b):
+        buf = (k_all, v_all)[which]
+        part = buf.at[aligned(2 * b + core, tok)]
+        return remote(part, part, kv_forwarded.at[which, b], kv_got.at[which, 2 * b + core],
+                      partner)
+
+    def kv_wait(which, source):
+        part = (k_all, v_all)[which].at[aligned(source, tok)]
+        pltpu.make_async_copy(part, part, kv_got.at[which, source]).wait()
+
+    for b in range(chips):
+        for which in range(2):
+            kv_wait(which, 2 * b + core)
+
+            @pl.when(chip != b)
+            def _():
+                forward(which, b).start()
+    for b in range(chips):
+        for which in range(2):
+            kv_wait(which, 2 * b + 1 - core)
     k_turned[...] = k_all[...].T
 
     def grad_copy(b, p):
@@ -196,13 +231,13 @@
         return jnp.dot(grads[aligned(d, rows), :], weights[:, aligned(k, cw)],
                        preferred_element_type=F32)
 
-    def set_out(d, buf, copy):
+    def set_out(d, buf, copy, first=0, end=None):
         def one(k, carry):
             buf[d, k] = product(d, k).astype(BF16)
             copy(d, k).start()
             return carry
 
-        lax.fori_loop(0, chunks, one, 0)
+        lax.fori_loop(first, chunks if end is None else end, one, 0)
 
     def pass_on(d, k, buf, copy):
         acc[...] = product(d, k)
@@ -230,6 +265,7 @@
             final_copy(k, 0).start()
             final_copy(k, 1).start()
 
+    early = chunks - chunks * 3 // 8
     for b in range(chips - 1, -1, -1):
         attend(b)
         if b == chips - 1:
@@ -246,41 +282,58 @@
         if b < chips - 1:
             @pl.when(chip == chips - 1)
             def _():
-                set_out(b, left_buf, left_copy)
+                set_out(b, left_buf, left_copy, 0, early if b == chips - 2 else chunks)
+
+    @pl.when(chip == chips - 1)
+    def _():
+        set_out(chips - 2, left_buf, left_copy, early, chunks)
 
     middle = (chip > 0) & (chip < chips - 1)
 
-    @pl.when(chip > 0)
+    @pl.when(middle)
     def _():
-        def one(i, carry):
+        def to_right(i, carry):
             pass_on(chips - 1 - i // chunks, i % chunks, right_buf, right_copy)
             return carry
 
-        lax.fori_loop(0, (chips - 1 - chip) * chunks, one, 0)
+        def to_left(i, carry):
+            pass_on(chip - 1 - i // chunks, i % chunks, left_buf, left_copy)
+            return carry
+
+        lax.fori_loop(0, (chip - 1) * chunks, to_left, 0)
+        lax.fori_loop(0, (chips - 1 - chip) * chunks, to_right, 0)
 
     def finish_one(k, carry):
         @pl.when(middle)
         def _():
-            pass_on(chip - 1, k, left_buf, left_copy)
-
-        finish(k)
+            pass_on(0, k, left_buf, left_copy)
+
+        @pl.when((chip != chips - 2) | (k < early))
+        def _():
+            finish(k)
+
         return carry
 
     lax.fori_loop(0, chunks, finish_one, 0)
 
-    @pl.when(middle)
+    @pl.when(chip == chips - 2)
     def _():
-        def one(i, carry):
-            pass_on(chip - 2 - i // chunks, i % chunks, left_buf, left_copy)
+        def one(k, carry):
+            finish(k)
             return carry
 
-        lax.fori_loop(0, (chip - 1) * chunks, one, 0)
+        lax.fori_loop(early, chunks, one, 0)
 
     def sent_both(copies):
         for copy in copies:
             copy.wait_send()
 
-    each_peer(lambda peer: sent_both(kv_copies(peer)))
+    each_twin(lambda peer: sent_both(kv_copies(peer)))
+    for b in range(chips):
+        @pl.when(chip != b)
+        def _():
+            forward(0, b).wait_send()
+            forward(1, b).wait_send()
     each_peer(lambda peer: sent_both(qo_copies(peer)))
     for b in range(chips):
         grad_copy(b, core).wait_send()
@@ -326,8 +379,6 @@
     rows = 2 * tok
     cw = min(256, width // 2)
     chunks = width // 2 // cw
-    ids = documents[0]
-    start = jnp.sum((ids[:, None] < ids[None, :]).astype(jnp.int32), axis=0, keepdims=True)
     dma = pltpu.SemaphoreType.DMA
     deep = 2 * feats + 4 * HD
     anywhere = pl.BlockSpec(memory_space=pl.ANY)
@@ -345,6 +396,7 @@
             pltpu.VMEM((HD, total), BF16),
             pltpu.VMEM((total, HD), F32),
             pltpu.VMEM((total, HD), F32),
+            pltpu.VMEM((1, total), jnp.int32),
             pltpu.VMEM((total, deep), BF16),
             pltpu.VMEM((deep, width // 2), BF16),
             pltpu.VMEM((chips, chunks, rows, cw), BF16),
@@ -357,7 +409,8 @@
             dma((count,)),
             dma((chips,)),
             dma((chips,)),
-            dma((2,)),
+            dma((2, count)),
+            dma((2, chips)),
             dma((5,)),
             dma((1,)),
             dma((1,)),
@@ -373,7 +426,7 @@
         compiler_params=pltpu.CompilerParams(
             collective_id=0, has_side_effects=True, vmem_limit_bytes=62 * 1024 * 1024),
         name="attention_back",
-    )(queries[0], keys[0], values[0], out_grad[0], start,
+    )(queries[0], keys[0], values[0], out_grad[0], documents,
       query_weight[0], key_weight[0], value_weight[0])
     return out[None]
 

time: 166 us -> 135 us (0.81)
  Pallas kernels: 161 us -> 133 us
  other arithmetic: 1.83 us -> 0 us
    pallas_call x1, Pallas kernels: 161 us -> 133 us  [body(): pl.pallas_call(functools.partial(kernel, (sections, count, tok, heads, wi...]
    reduce_sum x1 -> x0, other arithmetic: 1.83 us -> none  [body(): jnp.sum((ids[:, None] < ids[None, :]).astype(jnp.int32), axis=0, keepdims...]
where the time goes in v3:
time: 135 us
  Pallas kernels  133 us (99%)
  local copies, waits for them, and re-layouts  2.29 us (2%)
    pallas_call x1, Pallas kernels, body(): pl.pallas_call(functools.partial(kernel, (sections, count, tok, heads, wi...  133 us

profile of v3, /device:TPU:1, one launch (start us, length us, event | category | flops | bytes accessed | tf_op | source)
XLA Modules:
  0.0 134.9 jit_solution(3780707453988796868)
XLA Ops:
  0.0 132.6 %attention_back.1 = bf16[128,4096]{1,0:T(8,128)(2,1)} custom-call(bf16[128,4096]{1,0:T(8,128)(2,1)} %bitcast.12, bf16[128,512]{1,0:T(8,128)(2,1)} %bitcast.14, bf16[128,512]{1,0:T(8,128)(2,1)} %bitcast.15, bf16[128,4096]{1,0:T(8,128)(2,1)} %bitcast.13, s32[1,1024]{1,0:T(1,128)} %ids_ref.1, bf16[512,4096]{1,0:T(8,128)(2,1)} %bitcast.8, ...), custom_call_target="tpu_custom_call" | custom-call | tf_op jit(solution)/shard_map/attention_back/pallas_call | solution.py:386
  132.7 2.3 %copy.10 = bf16[1,128,4096]{2,1,0:T(8,128)(2,1)} copy(bf16[1,128,4096]{2,1,0:T(8,128)(2,1)} %bitcast.11) | data formatting | bytes 2097152
